TPU v7x, 32 devices: a whole 2x2x4 slice. The times are simulated.
32 devices in a mesh: tm: 8 (over z, y), series: 4 (over x, core).
Axes of the slice: x: 2, y: 2, z: 4, core: 2. Of those that a mesh axis runs over, the one named last changes fastest.
Arguments:
- signal: float32 [64, 262144], P('series', 'tm')
- valid_start: int32 [64], replicated, may hold values from 0 to 65535
- valid_end: int32 [64], replicated, may hold values from 196609 to 262144
Outputs:
- smooth: float32 [64, 262144], P('series', 'tm')
- slope: float32 [64, 262144], P('series', 'tm')
- covariance: float32 [64, 64], P('series')
Inputs may be any that keep to these rules, and one draw needn't show every extreme that they name: `valid_end`: end of the valid samples of each series.
All inputs are finite; a program needn't handle non-finite values.
Results may differ from a plain program's by a relative error of at most 0.00015.
Values sent between devices are 32-bit elements; how exact they have to be, the bound alone decides.
A program may use at most 64 MiB of HBM per device.

v0:
```python
import jax
import jax.numpy as jnp
from jax import lax
from jax.sharding import PartitionSpec as P

HALF = 16


def padded(cells, sides, width):
    for axis, dim in sides:
        count = lax.axis_size(axis)
        ends = count - 1
        head = lax.slice_in_dim(cells, 0, width, axis=dim)
        tail = lax.slice_in_dim(cells, cells.shape[dim] - width, cells.shape[dim], axis=dim)
        cells = jnp.concatenate(
            [
                lax.ppermute(tail, axis, [(i, (i + 1) % count) for i in range(ends)]),
                cells,
                lax.ppermute(head, axis, [((i + 1) % count, i) for i in range(ends)]),
            ],
            axis=dim,
        )
    return cells


def cross_rows(left, right):
    return lax.dot_general(
        left,
        right,
        (((1,), (1,)), ((), ())),
        precision=lax.Precision.HIGHEST,
        preferred_element_type=jnp.float32,
    )


def held_value(field, spot):
    return jnp.take_along_axis(field, spot, axis=1)


def shards(signal, valid_start, valid_end):
    rows, width = signal.shape
    taps = 2 * HALF + 1
    offsets = jnp.arange(-HALF, HALF + 1).astype(jnp.float32)
    second = jnp.sum(offsets * offsets)
    centre_sq = second / taps
    curved = offsets * offsets - centre_sq
    fourth = jnp.sum(curved * curved)
    extended = padded(signal, (("tm", 1),), 2 * HALF)
    span = width + 2 * HALF
    level = jnp.zeros((rows, span), jnp.float32)
    tilt = jnp.zeros((rows, span), jnp.float32)
    bend = jnp.zeros((rows, span), jnp.float32)
    for m in range(taps):
        window = extended[:, m : m + span]
        level = level + window * (1.0 / taps)
        tilt = tilt + window * (offsets[m] / second)
        bend = bend + window * (curved[m] / fourth)
    begin = lax.axis_index("tm") * width
    group = lax.axis_index("series") * rows
    first = lax.dynamic_slice_in_dim(valid_start, group, rows)[:, None]
    last = lax.dynamic_slice_in_dim(valid_end, group, rows)[:, None]
    moment = begin + jnp.arange(width, dtype=jnp.int32)[None, :]
    low_centre = first + HALF
    high_centre = last - HALF - 1
    centre = jnp.clip(moment, low_centre, high_centre)
    low_spot = jnp.clip(low_centre - begin + HALF, 0, span - 1)
    high_spot = jnp.clip(high_centre - begin + HALF, 0, span - 1)
    below = moment < low_centre
    above = moment > high_centre
    along = (moment - centre).astype(jnp.float32)
    lv = jnp.where(
        below,
        held_value(level, low_spot),
        jnp.where(above, held_value(level, high_spot), level[:, HALF : HALF + width]),
    )
    tl = jnp.where(
        below,
        held_value(tilt, low_spot),
        jnp.where(above, held_value(tilt, high_spot), tilt[:, HALF : HALF + width]),
    )
    bd = jnp.where(
        below,
        held_value(bend, low_spot),
        jnp.where(above, held_value(bend, high_spot), bend[:, HALF : HALF + width]),
    )
    inside = (moment >= first) & (moment < last)
    smooth = jnp.where(inside, lv + tl * along + bd * (along * along - centre_sq), 0.0)
    slope = jnp.where(inside, HALF * (tl + 2.0 * along * bd), 0.0)
    resid = jnp.where(inside, signal - smooth, 0.0)
    mixed = lax.all_to_all(resid, "series", split_axis=1, concat_axis=0, tiled=True)
    full = lax.psum(cross_rows(mixed, mixed), ("tm", "series"))
    gram = lax.dynamic_slice_in_dim(full, group, rows)
    correlation = (
        jnp.minimum(last, valid_end[None, :]) - jnp.maximum(first, valid_start[None, :])
    ).astype(jnp.float32)
    return (smooth, slope, gram / correlation)


def solution(mesh):
    in_specs = (P("series", "tm"), P(), P())
    out_specs = (P("series", "tm"), P("series", "tm"), P("series", None))
    return jax.shard_map(shards, mesh=mesh, in_specs=in_specs, out_specs=out_specs, check_vma=False)
```

profile of v0, /device:TPU:0, one launch (start us, length us, event | category | flops | bytes accessed | tf_op | source)
XLA Modules:
  0.0 258.8 jit_solution(5672851760717426179)
XLA Ops:
  0.6 0.8 fusion.14
  1.4 4.9 %collective-permute-start = (f32[16,32]{1,0:T(8,128)S(1)}, f32[16,32]{1,0:T(8,128)S(1)}, u32[]{:S(2)}, u32[]{:S(2)}) collective-permute-start(f32[16,32]{1,0:T(8,128)S(1)} %get-tuple-element.11), channel_id=1, source_target_pairs={{0,4},{4,8},{8,12},{12,16},{16,20},{20,24},{24,28},{1,5},{5,9},{9,... | collective-permute-start | bytes 6152 | tf_op jit(solution)/shard_map/ppermute | solution.py:17
  6.3 1.3 collective-permute-start.1
  7.6 0.6 multiply_reduce_fusion.1
  8.9 0.7 multiply_reduce_fusion
  9.6 0.7 fusion.18
  10.3 0.7 fusion.17
  11.0 0.7 fusion.16
  11.7 0.7 fusion.15
  12.4 0.0 copy-start.1
  12.4 3.1 %constant_dynamic-update-slice_fusion.1 = f32[16,32800]{1,0:T(8,128)} fusion(f32[16,32768]{1,0:T(8,128)} %param.5), kind=kLoop, calls=%fused_computation.27 | loop fusion | bytes 4194304
  15.5 0.1 broadcast_add_fusion.1
  15.6 0.1 broadcast_add_fusion
  103.3 0.3 dynamic-update-slice.2
  103.6 6.4 %dynamic-update-slice.3 = f32[16,32832]{1,0:T(8,128)S(1)} dynamic-update-slice(f32[16,32832]{1,0:T(8,128)S(1)} %dynamic-update-slice.2, f32[16,32768]{1,0:T(8,128)} %param.5, s32[]{} %constant.163, s32[]{} %constant.165) | dynamic-update-slice | bytes 4194308
  109.9 0.6 constant_dynamic-update-slice_fusion
  110.5 0.2 dynamic-update-slice.4
  110.7 19.9 %multiply_add_fusion.1 = f32[16,32800]{1,0:T(8,128)} fusion(f32[16,32800]{1,0:T(8,128)} %constant_dynamic-update-slice_fusion, f32[16,32832]{1,0:T(8,128)S(1)} %dynamic-update-slice.4, f32[16,32768]{1,0:T(8,128)} %param.5, f32[16,32]{1,0:T(8,128)S(1)} %collective-permute-done, f32[]{:T(128)S(6)} %div.236, f32[]{:T(128)S(6)} %div.235, f32[]{:T(128)S(6)} %div.234, ...), kind=kLoop, calls=%fused_computation.15 | loop fusion | flops 34636800 | bytes 71372928 | tf_op jit(solution)/shard_map/add | solution.py:56
  130.6 1.6 gather_fusion.3
  132.2 1.5 gather_fusion.2
  133.7 20.0 %add_multiply_fusion = f32[16,32800]{1,0:T(8,128)} fusion(f32[16,32800]{1,0:T(8,128)} %constant_dynamic-update-slice_fusion, f32[16,32832]{1,0:T(8,128)S(1)} %dynamic-update-slice.4, f32[16,32768]{1,0:T(8,128)} %param.5, f32[16,32]{1,0:T(8,128)S(1)} %collective-permute-done), kind=kLoop, calls=%fused_computation.13 | loop fusion | flops 17843200 | bytes 71372800 | tf_op jit(solution)/shard_map/add | solution.py:55
  153.8 1.6 gather_fusion.1
  155.4 1.5 gather_fusion
  156.9 19.9 %multiply_add_fusion = f32[16,32800]{1,0:T(8,128)} fusion(f32[16,32800]{1,0:T(8,128)} %constant_dynamic-update-slice_fusion, f32[16,32832]{1,0:T(8,128)S(1)} %dynamic-update-slice.4, f32[16,32768]{1,0:T(8,128)} %param.5, f32[16,32]{1,0:T(8,128)S(1)} %collective-permute-done, f32[]{:T(128)S(6)} %div.270, f32[]{:T(128)S(6)} %div.269, f32[]{:T(128)S(6)} %div.268, ...), kind=kLoop, calls=%fused_computation.14 | loop fusion | flops 34636800 | bytes 71372928 | tf_op jit(solution)/shard_map/add | solution.py:57
  176.8 1.6 gather_fusion.5
  178.4 1.5 gather_fusion.4
  180.0 6.0 %subtract_select_fusion = (f32[16,32768]{1,0:T(8,128)S(1)}, f32[16,32768]{1,0:T(8,128)}, f32[16,32768]{1,0:T(8,128)}) fusion(f32[16,32768]{1,0:T(8,128)} %param.5, s32[32768]{0:T(1024)S(1)} %iota_add_fusion, s32[16]{0:T(128)S(1)} %get-tuple-element.9, s32[16]{0:T(128)S(1)} %get-tuple-element.7, f32[]{:T(128)S(6)} %div.237, f32[16,32800]{1,0:T(8,128)} %multiply_add_fusion, ...), kind=kLoop, calls=%fused_computation.20 | loop fusion | flops 15204352 | bytes 14811780 | tf_op jit(solution)/shard_map/jit(_where)/select_n | solution.py:89
  186.0 0.1 copy.9
  186.1 28.3 %all_to_all.19 = f32[16,4,8192]{2,0,1:T(8,128)S(1)} all-to-all(f32[16,4,8192]{2,0,1:T(8,128)S(1)} %bitcast.161), channel_id=1, replica_groups=mesh['tm'=8,'series'=4] {'series'}, dimensions={1} | all-to-all | bytes 4194304 | tf_op jit(solution)/shard_map/all_to_all | solution.py:90
  214.5 1.8 fusion.19
  216.2 41.9 %psum.7 = f32[64,64]{1,0:T(8,128)S(1)} all-reduce(f32[64,64]{1,0:T(8,128)S(1)} %fusion.19), channel_id=1, replica_groups=mesh['tm'=8,'series'=4] {'tm','series'}, use_global_device_ids=true, to_apply=%region_2.4 | all-reduce | flops 4096 | bytes 32768 | tf_op jit(solution)/shard_map/psum | solution.py:91
  258.1 0.7 convert_divide_fusion
  (16 shorter events, 0.1 us)
Async XLA Ops:
  1.4 101.8 %collective-permute-start = (f32[16,32]{1,0:T(8,128)S(1)}, f32[16,32]{1,0:T(8,128)S(1)}, u32[]{:S(2)}, u32[]{:S(2)}) collective-permute-start(f32[16,32]{1,0:T(8,128)S(1)} %get-tuple-element.11), channel_id=1, source_target_pairs={{0,4},{4,8},{8,12},{12,16},{16,20},{20,24},{24,28},{1,5},{5,9},{9,... | collective-permute-start | bytes 6152 | tf_op jit(solution)/shard_map/ppermute | solution.py:17
  6.3 103.6 %collective-permute-start.1 = (f32[16,32]{1,0:T(8,128)S(1)}, f32[16,32]{1,0:T(8,128)S(1)}, u32[]{:S(2)}, u32[]{:S(2)}) collective-permute-start(f32[16,32]{1,0:T(8,128)S(1)} %get-tuple-element.12), channel_id=1, source_target_pairs={{4,0},{8,4},{12,8},{16,12},{20,16},{24,20},{28,24},{5,1},{9,5},{13... | collective-permute-start | bytes 6152 | tf_op jit(solution)/shard_map/ppermute | solution.py:19
  12.4 3.1 %copy-start.1 = (s32[64]{0:T(128)S(1)}, s32[64]{0:T(128)}, u32[]{:S(2)}) copy-start(s32[64]{0:T(128)} %param.6) | copy-start | bytes 772
  12.4 3.2 %copy-start = (s32[64]{0:T(128)S(1)}, s32[64]{0:T(128)}, u32[]{:S(2)}) copy-start(s32[64]{0:T(128)} %param.7) | copy-start | bytes 772
where the time goes:
time: 261 us; the launch traced here: 259 us
  between operations  88.9 us (34%)
  blocking collectives  70.2 us (27%)
  other arithmetic  68 us (26%)
  local copies, waits for them, and re-layouts  23.7 us (9%)
  starting transfers between devices  6.18 us (2%)
    psum x1, blocking collectives, shards(): full = lax.psum(cross_rows(mixed, mixed), ('tm', 'series'))  41.9 us
    all_to_all x1, blocking collectives, shards(): lax.all_to_all(resid, 'series', split_axis=1, concat_axis=0, tiled=True)  28.3 us
    add x1, other arithmetic, shards(): level = level + window * (1.0 / taps)  20 us
    add x1, other arithmetic, shards(): tilt = tilt + window * (offsets[m] / second)  19.9 us
    add x1, other arithmetic, shards(): bend = bend + window * (curved[m] / fourth)  19.9 us
    unnamed x7, local copies, waits for them, and re-layouts  9.73 us
    gather x6, local copies, waits for them, and re-layouts, held_value(): return jnp.take_along_axis(field, spot, axis=1)  9.45 us
    select_n x1, other arithmetic, shards(): resid = jnp.where(inside, signal - smooth, 0.0)  5.98 us
  transfers between devices with their start and end apart: 2, of which 0 were waited for; matrix products, arithmetic and copies ran while one was open for 5% of the time, Pallas kernels for 0%

commit v1 on v0

--- a/solution.py
+++ b/solution.py
@@ -87,7 +87,12 @@
     smooth = jnp.where(inside, lv + tl * along + bd * (along * along - centre_sq), 0.0)
     slope = jnp.where(inside, HALF * (tl + 2.0 * along * bd), 0.0)
     resid = jnp.where(inside, signal - smooth, 0.0)
-    mixed = lax.all_to_all(resid, "series", split_axis=1, concat_axis=0, tiled=True)
+    mixed = jnp.concatenate(
+        lax.all_to_all(
+            jnp.stack(jnp.split(resid, lax.axis_size("series"), axis=1)), "series", 0, 0
+        ),
+        axis=0,
+    )
     full = lax.psum(cross_rows(mixed, mixed), ("tm", "series"))
     gram = lax.dynamic_slice_in_dim(full, group, rows)
     correlation = (

time: 261 us -> 261 us (level)
  no operation moved by 1% of the time
where the time goes in v1:
time: 261 us; the launch traced here: 259 us
  between operations  88.8 us (34%)
  blocking collectives  70.2 us (27%)
  other arithmetic  68.1 us (26%)
  local copies, waits for them, and re-layouts  23.8 us (9%)
  starting transfers between devices  6.18 us (2%)
    psum x1, blocking collectives, shards(): full = lax.psum(cross_rows(mixed, mixed), ('tm', 'series'))  41.9 us
    all_to_all x1, blocking collectives, shards(): lax.all_to_all(jnp.stack(jnp.split(resid, lax.axis_size('series'), axis=1...  28.4 us
    add x1, other arithmetic, shards(): level = level + window * (1.0 / taps)  20 us
    add x1, other arithmetic, shards(): tilt = tilt + window * (offsets[m] / second)  19.9 us
    add x1, other arithmetic, shards(): bend = bend + window * (curved[m] / fourth)  19.9 us
    unnamed x7, local copies, waits for them, and re-layouts  9.75 us
    gather x6, local copies, waits for them, and re-layouts, held_value(): return jnp.take_along_axis(field, spot, axis=1)  9.46 us
    select_n x1, other arithmetic, shards(): resid = jnp.where(inside, signal - smooth, 0.0)  5.98 us
  transfers between devices with their start and end apart: 2, of which 0 were waited for; matrix products, arithmetic and copies ran while one was open for 5% of the time, Pallas kernels for 0%

profile of v1, /device:TPU:0, one launch (start us, length us, event | category | flops | bytes accessed | tf_op | source)
XLA Modules:
  0.0 258.9 jit_solution(16074832601618632375)
XLA Ops:
  0.6 0.8 fusion.14
  1.4 4.9 %collective-permute-start = (f32[16,32]{1,0:T(8,128)S(1)}, f32[16,32]{1,0:T(8,128)S(1)}, u32[]{:S(2)}, u32[]{:S(2)}) collective-permute-start(f32[16,32]{1,0:T(8,128)S(1)} %get-tuple-element.15), channel_id=1, source_target_pairs={{0,4},{4,8},{8,12},{12,16},{16,20},{20,24},{24,28},{1,5},{5,9},{9,... | collective-permute-start | bytes 6152 | tf_op jit(solution)/shard_map/ppermute | solution.py:17
  6.3 1.3 collective-permute-start.1
  7.6 0.6 multiply_reduce_fusion.1
  8.9 0.7 multiply_reduce_fusion
  9.6 0.7 fusion.18
  10.3 0.7 fusion.17
  11.0 0.7 fusion.16
  11.7 0.7 fusion.15
  12.4 3.1 %constant_dynamic-update-slice_fusion.1 = f32[16,32800]{1,0:T(8,128)} fusion(f32[16,32768]{1,0:T(8,128)} %param.5), kind=kLoop, calls=%fused_computation.31 | loop fusion | bytes 4194304
  15.6 0.1 broadcast_add_fusion.1
  15.7 0.1 broadcast_add_fusion
  103.2 0.3 dynamic-update-slice.2
  103.5 6.4 %dynamic-update-slice.3 = f32[16,32832]{1,0:T(8,128)S(1)} dynamic-update-slice(f32[16,32832]{1,0:T(8,128)S(1)} %dynamic-update-slice.2, f32[16,32768]{1,0:T(8,128)} %param.5, s32[]{} %constant.164, s32[]{} %constant.166) | dynamic-update-slice | bytes 4194308
  109.9 0.6 constant_dynamic-update-slice_fusion
  110.5 0.2 dynamic-update-slice.4
  110.6 19.9 %multiply_add_fusion.1 = f32[16,32800]{1,0:T(8,128)} fusion(f32[16,32800]{1,0:T(8,128)} %constant_dynamic-update-slice_fusion, f32[16,32832]{1,0:T(8,128)S(1)} %dynamic-update-slice.4, f32[16,32768]{1,0:T(8,128)} %param.5, f32[16,32]{1,0:T(8,128)S(1)} %collective-permute-done, f32[]{:T(128)S(6)} %div.236, f32[]{:T(128)S(6)} %div.235, f32[]{:T(128)S(6)} %div.234, ...), kind=kLoop, calls=%fused_computation.15 | loop fusion | flops 34636800 | bytes 71372928 | tf_op jit(solution)/shard_map/add | solution.py:56
  130.5 1.6 gather_fusion.3
  132.2 1.5 gather_fusion.2
  133.7 20.0 %add_multiply_fusion = f32[16,32800]{1,0:T(8,128)} fusion(f32[16,32800]{1,0:T(8,128)} %constant_dynamic-update-slice_fusion, f32[16,32832]{1,0:T(8,128)S(1)} %dynamic-update-slice.4, f32[16,32768]{1,0:T(8,128)} %param.5, f32[16,32]{1,0:T(8,128)S(1)} %collective-permute-done), kind=kLoop, calls=%fused_computation.13 | loop fusion | flops 17843200 | bytes 71372800 | tf_op jit(solution)/shard_map/add | solution.py:55
  153.7 1.6 gather_fusion.1
  155.3 1.5 gather_fusion
  156.9 19.9 %multiply_add_fusion = f32[16,32800]{1,0:T(8,128)} fusion(f32[16,32800]{1,0:T(8,128)} %constant_dynamic-update-slice_fusion, f32[16,32832]{1,0:T(8,128)S(1)} %dynamic-update-slice.4, f32[16,32768]{1,0:T(8,128)} %param.5, f32[16,32]{1,0:T(8,128)S(1)} %collective-permute-done, f32[]{:T(128)S(6)} %div.270, f32[]{:T(128)S(6)} %div.269, f32[]{:T(128)S(6)} %div.268, ...), kind=kLoop, calls=%fused_computation.14 | loop fusion | flops 34636800 | bytes 71372928 | tf_op jit(solution)/shard_map/add | solution.py:57
  176.7 1.6 gather_fusion.5
  178.4 1.5 gather_fusion.4
  179.9 6.0 %subtract_select_fusion = (f32[16,32768]{1,0:T(8,128)S(1)}, f32[16,32768]{1,0:T(8,128)}, f32[16,32768]{1,0:T(8,128)}) fusion(f32[16,32768]{1,0:T(8,128)} %param.5, s32[32768]{0:T(1024)S(1)} %iota_add_fusion, s32[16]{0:T(128)S(1)} %get-tuple-element.9, s32[16]{0:T(128)S(1)} %get-tuple-element.7, f32[]{:T(128)S(6)} %div.237, f32[16,32800]{1,0:T(8,128)} %multiply_add_fusion, ...), kind=kLoop, calls=%fused_computation.20 | loop fusion | flops 15204352 | bytes 14811780 | tf_op jit(solution)/shard_map/jit(_where)/select_n | solution.py:89
  185.9 0.1 slice_bitcast_fusion.3
  186.0 0.1 pad_maximum_fusion.1
  186.2 28.4 %all_to_all.5 = f32[4,16,8192]{2,1,0:T(8,128)S(1)} all-to-all(f32[4,16,8192]{2,1,0:T(8,128)S(1)} %pad_maximum_fusion.1), channel_id=1, replica_groups=mesh['tm'=8,'series'=4] {'series'}, dimensions={0} | all-to-all | bytes 4194304 | tf_op jit(solution)/shard_map/all_to_all | solution.py:91
  214.5 1.8 fusion.19
  216.3 41.9 %psum.7 = f32[64,64]{1,0:T(8,128)S(1)} all-reduce(f32[64,64]{1,0:T(8,128)S(1)} %fusion.19), channel_id=1, replica_groups=mesh['tm'=8,'series'=4] {'tm','series'}, use_global_device_ids=true, to_apply=%region_2.4 | all-reduce | flops 4096 | bytes 32768 | tf_op jit(solution)/shard_map/psum | solution.py:96
  258.2 0.7 convert_divide_fusion
  (17 shorter events, 0.1 us)
Async XLA Ops:
  1.4 101.8 %collective-permute-start = (f32[16,32]{1,0:T(8,128)S(1)}, f32[16,32]{1,0:T(8,128)S(1)}, u32[]{:S(2)}, u32[]{:S(2)}) collective-permute-start(f32[16,32]{1,0:T(8,128)S(1)} %get-tuple-element.15), channel_id=1, source_target_pairs={{0,4},{4,8},{8,12},{12,16},{16,20},{20,24},{24,28},{1,5},{5,9},{9,... | collective-permute-start | bytes 6152 | tf_op jit(solution)/shard_map/ppermute | solution.py:17
  6.3 103.5 %collective-permute-start.1 = (f32[16,32]{1,0:T(8,128)S(1)}, f32[16,32]{1,0:T(8,128)S(1)}, u32[]{:S(2)}, u32[]{:S(2)}) collective-permute-start(f32[16,32]{1,0:T(8,128)S(1)} %get-tuple-element.16), channel_id=1, source_target_pairs={{4,0},{8,4},{12,8},{16,12},{20,16},{24,20},{28,24},{5,1},{9,5},{13... | collective-permute-start | bytes 6152 | tf_op jit(solution)/shard_map/ppermute | solution.py:19
  12.4 3.1 %copy-start.1 = (s32[64]{0:T(128)S(1)}, s32[64]{0:T(128)}, u32[]{:S(2)}) copy-start(s32[64]{0:T(128)} %param.6) | copy-start | bytes 772
  12.4 3.2 %copy-start = (s32[64]{0:T(128)S(1)}, s32[64]{0:T(128)}, u32[]{:S(2)}) copy-start(s32[64]{0:T(128)} %param.7) | copy-start | bytes 772
